TPU v7x, 32 devices: a whole 2x2x4 slice. The times are simulated.
32 devices in a mesh: heads: 4 (over x, core), ctx: 8 (over z, y).
Axes of the slice: x: 2, y: 2, z: 4, core: 2. Of those that a mesh axis runs over, the one named last changes fastest.
Arguments:
- queries: bfloat16 [1536, 2048], P('ctx', 'heads'), may hold values from -6 to 6
- key_states: bfloat16 [1536, 512], P('ctx', 'heads'), may hold values from -6 to 6
- value_states: bfloat16 [1536, 512], P('ctx', 'heads'), may hold values from -6 to 6
- attention_out: bfloat16 [1536, 2048], P('ctx', 'heads'), may hold values from -2 to 2
- out_grad: bfloat16 [1536, 2048], P('ctx', 'heads'), may hold values from -6 to 6
- log_sum_exp: float32 [16, 1536], P('heads', 'ctx'), may hold values from 0 to 16, as said below
- block_counts: int32 [8], replicated, may hold values from 1 to 3, as said below
- w_query: bfloat16 [4096, 2048], P(None, 'heads'), may hold values from -0.09375 to 0.09375
- w_key: bfloat16 [4096, 512], P(None, 'heads'), may hold values from -0.09375 to 0.09375
- w_value: bfloat16 [4096, 512], P(None, 'heads'), may hold values from -0.09375 to 0.09375
Outputs:
- input_grad: bfloat16 [1536, 4096], P('ctx', 'heads')
- key_grad: float32 [1536, 512], P('ctx', 'heads')
- value_grad: float32 [1536, 512], P('ctx', 'heads')
Inputs may be any that keep to these rules, and one draw needn't show every extreme that they name: `block_counts`: one entry equals 3. `log_sum_exp`: finite offsets of each row's scores.
All inputs are finite; a program needn't handle non-finite values.
Results may differ from a plain program's by a relative error of at most 0.0063.
Values may be sent and summed in bfloat16 or wider, within the bound.
A program may use at most 128 MiB of HBM per device.

v0:
```python
import math

import jax
import jax.numpy as jnp
from jax import lax
from jax.sharding import PartitionSpec as P

BLOCK = 64


def key_span(row_count, capacity):
    shards = row_count // capacity
    per_step = max(1, min(shards, 512 // capacity))
    while shards % per_step:
        per_step = per_step - 1
    return per_step * capacity


def row_info(row_index, lengths, offsets, capacity):
    device = row_index // capacity
    onehot = device[:, None] == jnp.arange(lengths.shape[0], dtype=jnp.int32)[None, :]
    length = jnp.sum(jnp.where(onehot, lengths[None, :], 0), axis=1)
    offset = jnp.sum(jnp.where(onehot, offsets[None, :], 0), axis=1)
    within = row_index - device * capacity
    return (offset + within, within < length)


def tile_grads(
    query_blk,
    grad_blk,
    norm_blk,
    delta_blk,
    query_pos,
    query_live,
    key_blk,
    value_blk,
    key_pos,
    key_live,
    score_scale,
):
    scores = (
        jnp.einsum("qgd,kd->gqk", query_blk, key_blk, preferred_element_type=jnp.float32)
        * score_scale
    )
    visible = query_live[:, None] & key_live[None, :] & (key_pos[None, :] <= query_pos[:, None])
    probability = jnp.where(visible[None], jnp.exp(scores - norm_blk.T[:, :, None]), 0.0)
    prob_grad = jnp.einsum("qgd,kd->gqk", grad_blk, value_blk, preferred_element_type=jnp.float32)
    score_grad = probability * (prob_grad - delta_blk.T[:, :, None])
    return (probability.astype(jnp.bfloat16), score_grad.astype(jnp.bfloat16))


def on_device(
    queries,
    key_states,
    value_states,
    attention_out,
    out_grad,
    log_sum_exp,
    block_counts,
    w_query,
    w_key,
    w_value,
):
    capacity = key_states.shape[0]
    head_dim = key_states.shape[1]
    group = queries.shape[1] // head_dim
    score_scale = 1.0 / math.sqrt(head_dim)
    own_index = lax.axis_index("ctx")
    lengths = block_counts * BLOCK
    offsets = jnp.cumsum(lengths) - lengths
    own_rows = own_index * capacity + jnp.arange(capacity, dtype=jnp.int32)
    own_pos, own_live = row_info(own_rows, lengths, offsets, capacity)
    query_heads = queries.reshape(capacity, group, head_dim)
    grad_heads = out_grad.reshape(capacity, group, head_dim)
    output_heads = attention_out.reshape(capacity, group, head_dim)
    delta_rows = jnp.sum(grad_heads.astype(jnp.float32) * output_heads.astype(jnp.float32), axis=2)
    norm_rows = log_sum_exp.T
    zero_rows = jnp.zeros((capacity, group, head_dim), jnp.float32)
    zero_own = jnp.zeros((capacity, head_dim), jnp.float32)
    key_piece = lax.all_gather(key_states, "ctx", axis=0, tiled=True)
    value_piece = lax.all_gather(value_states, "ctx", axis=0, tiled=True)
    span = key_span(key_piece.shape[0], capacity)

    def step(block_num, query_grad):
        begin_row = block_num * span
        key_blk = lax.dynamic_slice_in_dim(key_piece, begin_row, span, 0)
        value_blk = lax.dynamic_slice_in_dim(value_piece, begin_row, span, 0)
        key_pos, key_live = row_info(
            begin_row + jnp.arange(span, dtype=jnp.int32), lengths, offsets, capacity
        )

        def compute():
            prob_b, grad_b = tile_grads(
                query_heads,
                grad_heads,
                norm_rows,
                delta_rows,
                own_pos,
                own_live,
                key_blk,
                value_blk,
                key_pos,
                key_live,
                score_scale,
            )
            return score_scale * jnp.einsum(
                "gqk,kd->qgd", grad_b, key_blk, preferred_element_type=jnp.float32
            )

        terms = compute()
        return query_grad + terms

    query_grad = lax.fori_loop(0, key_piece.shape[0] // span, step, zero_rows)
    norm_all, delta_all = (
        lax.all_gather(norm_rows, "ctx", axis=0, tiled=True),
        lax.all_gather(delta_rows, "ctx", axis=0, tiled=True),
    )
    query_piece = lax.all_gather(queries, "ctx", axis=0, tiled=True)
    grad_piece = lax.all_gather(out_grad, "ctx", axis=0, tiled=True)
    fold_span = key_span(query_piece.shape[0], capacity)

    def step(block_num, state):
        key_acc, value_acc = state
        begin_row = block_num * fold_span
        query_blk = lax.dynamic_slice_in_dim(query_piece, begin_row, fold_span, 0).reshape(
            fold_span, group, head_dim
        )
        grad_blk = lax.dynamic_slice_in_dim(grad_piece, begin_row, fold_span, 0).reshape(
            fold_span, group, head_dim
        )
        norm_blk = lax.dynamic_slice_in_dim(norm_all, begin_row, fold_span, 0)
        delta_blk = lax.dynamic_slice_in_dim(delta_all, begin_row, fold_span, 0)
        query_pos, query_live = row_info(
            begin_row + jnp.arange(fold_span, dtype=jnp.int32), lengths, offsets, capacity
        )

        def compute():
            prob_b, grad_b = tile_grads(
                query_blk,
                grad_blk,
                norm_blk,
                delta_blk,
                query_pos,
                query_live,
                key_states,
                value_states,
                own_pos,
                own_live,
                score_scale,
            )
            return (
                score_scale
                * jnp.einsum("gqk,qgd->kd", grad_b, query_blk, preferred_element_type=jnp.float32),
                jnp.einsum("gqk,qgd->kd", prob_b, grad_blk, preferred_element_type=jnp.float32),
            )

        terms = compute()
        return (key_acc + terms[0], value_acc + terms[1])

    key_grad, value_grad = lax.fori_loop(
        0, query_piece.shape[0] // fold_span, step, (zero_own, zero_own)
    )
    query_flat = query_grad.reshape(capacity, group * head_dim).astype(jnp.bfloat16)
    partial_input = jnp.einsum("rc,mc->rm", query_flat, w_query, preferred_element_type=jnp.float32)
    partial_input = partial_input + jnp.einsum(
        "rc,mc->rm", key_grad.astype(jnp.bfloat16), w_key, preferred_element_type=jnp.float32
    )
    partial_input = partial_input + jnp.einsum(
        "rc,mc->rm", value_grad.astype(jnp.bfloat16), w_value, preferred_element_type=jnp.float32
    )
    input_part = lax.psum_scatter(partial_input, "heads", scatter_dimension=1, tiled=True)
    return (input_part.astype(jnp.bfloat16), key_grad, value_grad)


def solution(mesh):
    return jax.shard_map(
        on_device,
        mesh=mesh,
        in_specs=(
            P("ctx", "heads"),
            P("ctx", "heads"),
            P("ctx", "heads"),
            P("ctx", "heads"),
            P("ctx", "heads"),
            P("heads", "ctx"),
            P(),
            P(None, "heads"),
            P(None, "heads"),
            P(None, "heads"),
        ),
        out_specs=(P("ctx", "heads"), P("ctx", "heads"), P("ctx", "heads")),
        check_vma=False,
    )
```

profile of v0, /device:TPU:0, one launch (start us, length us, event | category | flops | bytes accessed | tf_op | source)
XLA Modules:
  0.0 253.6 jit_solution(5064324992087366843)
XLA Ops:
  8.7 1.0 reshape.280
  9.7 1.0 copy_bitcast_fusion
  12.7 0.7 select_reduce_fusion.4
  15.1 34.2 %all_gather.18 = bf16[1536,128]{1,0:T(8,128)(2,1)S(1)} all-gather(bf16[192,128]{1,0:T(8,128)(2,1)} %param.15), channel_id=1, replica_groups=mesh['heads'=4,'ctx'=8] {'ctx'}, dimensions={0}, use_global_device_ids=true | all-gather | bytes 442368 | tf_op jit(solution)/shard_map/all_gather | solution.py:80
  49.3 33.4 %all_gather.19 = bf16[1536,128]{1,0:T(8,128)(2,1)} all-gather(bf16[192,128]{1,0:T(8,128)(2,1)S(1)} %copy-done.3), channel_id=1, replica_groups=mesh['heads'=4,'ctx'=8] {'ctx'}, dimensions={0}, use_global_device_ids=true | all-gather | bytes 442368 | tf_op jit(solution)/shard_map/all_gather | solution.py:81
  82.7 18.1 %while.34 = (s32[]{:T(128)}, f32[192,4,128]{2,0,1:T(8,128)S(1)}, bf16[1536,128]{1,0:T(8,128)(2,1)S(1)}, pred[192]{0:T(512)(128)(4,1)}, s32[8]{0:T(128)}, /*index...) while((s32[]{:T(128)}, f32[192,4,128]{2,0,1:T(8,128)S(1)}, ...), condition=%wide.region_7.8_spmd.clone, body=%wide.region_4.7_spmd.clone.sunk | while | flops 228805248 | bytes 4005340 | solution.py:113
  83.5 0.8 compare_and_fusion.4
  84.3 1.4 fusion.93
  85.7 1.5 fusion.94
  87.3 0.7 select_reduce_fusion.8
  88.0 0.8 compare_and_fusion.4
  88.8 1.4 fusion.93
  90.2 1.5 fusion.94
  92.5 0.8 compare_and_fusion.4
  93.4 1.4 fusion.93
  94.7 1.5 fusion.94
  97.1 0.8 compare_and_fusion.4
  97.9 1.4 fusion.93
  99.3 1.5 fusion.94
  100.9 30.6 %all-gather.1 = f32[8,192,4]{1,2,0:T(4,128)S(1)} all-gather(f32[1,192,4]{1,2,0:T(4,128)S(1)} %copy.55), channel_id=1, replica_groups=mesh['heads'=4,'ctx'=8] {'ctx'}, dimensions={0}, use_global_device_ids=true | all-gather | bytes 27648 | tf_op jit(solution)/shard_map/all_gather | solution.py:116
  132.3 30.6 %all-gather = f32[8,192,4]{1,2,0:T(4,128)S(1)} all-gather(f32[1,192,4]{1,2,0:T(4,128)S(1)} %bitcast.173), channel_id=1, replica_groups=mesh['heads'=4,'ctx'=8] {'ctx'}, dimensions={0}, use_global_device_ids=true | all-gather | bytes 27648 | tf_op jit(solution)/shard_map/all_gather | solution.py:115
  163.6 5.4 %fusion.46 = f32[192,4096]{1,0:T(8,128)} fusion(bf16[4096,512]{1,0:T(8,128)(2,1)} %param.21, f32[192,4,128]{2,0,1:T(8,128)S(1)} %get-tuple-element.600), kind=kOutput, calls=%fused_computation.72 | convolution fusion | flops 805404672 | bytes 7733248 | tf_op jit(solution)/shard_map/rc,mc->rm/dot_general | solution.py:164
  168.9 31.9 %while.35 = (s32[]{:T(128)}, f32[192,128]{1,0:T(8,128)S(1)}, f32[192,128]{1,0:T(8,128)}, s32[8]{0:T(128)}, pred[192]{0:T(512)(128)(4,1)}, /*index=5*/s32[192]{0:...) while((s32[]{:T(128)}, f32[192,128]{1,0:T(8,128)S(1)}, ...), condition=%wide.region_11.12_spmd.clone, body=%wide.region_8.11_spmd.clone.sunk | while | flops 304425600 | bytes 8972294 | solution.py:160
  169.7 0.8 compare_and_fusion.5
  170.5 1.2 constant_dynamic-slice_fusion.3
  171.9 1.3 dynamic-slice_bitcast_fusion.3
  173.2 1.2 fusion.104
  174.6 1.0 fusion.106
  177.0 0.8 compare_and_fusion.5
  177.8 1.2 constant_dynamic-slice_fusion.3
  179.2 1.3 dynamic-slice_bitcast_fusion.3
  180.5 1.2 fusion.104
  182.0 1.9 fusion.106
  185.2 0.8 compare_and_fusion.5
  186.0 1.2 constant_dynamic-slice_fusion.3
  187.4 1.3 dynamic-slice_bitcast_fusion.3
  188.7 1.2 fusion.104
  190.2 1.9 fusion.106
  192.7 0.7 select_reduce_fusion.9
  193.4 0.8 compare_and_fusion.5
  194.3 1.2 constant_dynamic-slice_fusion.3
  195.6 1.3 dynamic-slice_bitcast_fusion.3
  196.9 1.2 fusion.104
  198.4 1.9 fusion.106
  200.9 2.6 %convolution_add_fusion.1 = f32[192,4096]{1,0:T(8,128)S(1)} fusion(f32[192,4096]{1,0:T(8,128)} %fusion.46, bf16[4096,128]{1,0:T(8,128)(2,1)S(1)} %copy-done, f32[192,128]{1,0:T(8,128)S(1)} %get-tuple-element.598), kind=kOutput, calls=%fused_computation.70 | convolution fusion | flops 202137600 | bytes 7438336 | tf_op jit(solution)/shard_map/rc,mc->rm/dot_general | solution.py:165
  203.5 2.2 convolution_add_fusion
  205.8 39.4 %reduce-scatter.2.cloned.1.call-done = f32[192,1024]{1,0:T(8,128)} async-done(((f32[192,4096]{1,0:T(8,128)}), f32[192,1024]{1,0:T(8,128)}) %reduce-scatter.2.cloned.1.call-update) | async-done | bytes 786448 | tf_op jit(solution)/shard_map/reduce_scatter | solution.py:171
  245.1 1.9 convert_element_type.61
  (94 shorter events, 15.4 us)
Async XLA Ops:
  7.2 193.7 %copy-start = (bf16[4096,128]{1,0:T(8,128)(2,1)S(1)}, bf16[4096,128]{1,0:T(8,128)(2,1)}, u32[]{:S(2)}) copy-start(bf16[4096,128]{1,0:T(8,128)(2,1)} %param.22) | copy-start | bytes 3145732
  7.2 3.5 %copy-start.5 = (bf16[192,512]{1,0:T(8,128)(2,1)S(1)}, bf16[192,512]{1,0:T(8,128)(2,1)}, u32[]{:S(2)}) copy-start(bf16[192,512]{1,0:T(8,128)(2,1)} %param.14) | copy-start | bytes 589828
  7.2 4.2 %copy-start.9 = (s32[8]{0:T(128)S(1)}, s32[8]{0:T(128)}, u32[]{:S(2)}) copy-start(s32[8]{0:T(128)} %param.20) | copy-start | bytes 100
  7.2 7.4 %copy-start.7 = (bf16[192,512]{1,0:T(8,128)(2,1)S(1)}, bf16[192,512]{1,0:T(8,128)(2,1)}, u32[]{:S(2)}) copy-start(bf16[192,512]{1,0:T(8,128)(2,1)} %param.17) | copy-start | bytes 589828
  7.2 161.7 %all-gather.5.cloned.1.call-start = ((), (), s32[]{:S(2)}) async-start(), calls=%async_computation.1 | async-start | bytes 1769472 | tf_op jit(solution)/shard_map/all_gather | solution.py:118
  7.9 161.0 %all-gather.7.cloned.1.call-start = ((), (), s32[]{:S(2)}) async-start(), calls=%async_computation.2 | async-start | bytes 1769472 | tf_op jit(solution)/shard_map/all_gather | solution.py:119
  8.7 236.4 %reduce-scatter.2.cloned.1.call-start = ((), (), s32[]{:S(2)}) async-start(), calls=%async_computation.3 | async-start | bytes 3932160 | tf_op jit(solution)/shard_map/reduce_scatter | solution.py:171
  10.7 38.6 %copy-start.3 = (bf16[192,128]{1,0:T(8,128)(2,1)S(1)}, bf16[192,128]{1,0:T(8,128)(2,1)}, u32[]{:S(2)}) copy-start(bf16[192,128]{1,0:T(8,128)(2,1)} %param.16) | copy-start | bytes 147460
  11.4 71.3 %copy-start.8 = (f32[4,192]{1,0:T(4,128)S(1)}, f32[4,192]{1,0:T(4,128)}, u32[]{:S(2)}) copy-start(f32[4,192]{1,0:T(4,128)} %param.19) | copy-start | bytes 9220
  174.6 1.0 copy-start.6
  181.9 1.9 copy-start.6
  190.2 1.9 copy-start.6
  198.4 1.9 copy-start.6
  200.9 2.6 %copy-start.1 = (f32[192,128]{1,0:T(8,128)}, f32[192,128]{1,0:T(8,128)S(1)}, u32[]{:S(2)}) copy-start(f32[192,128]{1,0:T(8,128)S(1)} %get-tuple-element.598) | copy-start | bytes 294916
  200.9 2.6 %copy-start.2 = (f32[192,128]{1,0:T(8,128)S(1)}, f32[192,128]{1,0:T(8,128)}, u32[]{:S(2)}) copy-start(f32[192,128]{1,0:T(8,128)} %get-tuple-element.599) | copy-start | bytes 294916
  200.9 2.6 %copy-start.4 = (bf16[4096,128]{1,0:T(8,128)(2,1)S(1)}, bf16[4096,128]{1,0:T(8,128)(2,1)}, u32[]{:S(2)}) copy-start(bf16[4096,128]{1,0:T(8,128)(2,1)} %param.23) | copy-start | bytes 3145732
Sparse Core Ops, SparseCore 0:
  10.2 50.6 all-gather.4
  63.1 43.6 all-gather.6
  205.9 39.1 reduce-scatter.1
where the time goes:
time: 255 us; the launch traced here: 254 us
  blocking collectives  129 us (51%)
  waiting for transfers between devices  40.8 us (16%)
  matrix products  35.5 us (14%)
  other arithmetic  18 us (7%)
  local copies, waits for them, and re-layouts  16 us (6%)
  between operations  13.9 us (5%)
    reduce_scatter x1, waiting for transfers between devices, on_device(): lax.psum_scatter(partial_input, 'heads', scatter_dimension=1, tiled=True)  39.4 us
    all_gather x1, blocking collectives, on_device(): key_piece = lax.all_gather(key_states, 'ctx', axis=0, tiled=True)  34.2 us
    all_gather x1, blocking collectives, on_device(): value_piece = lax.all_gather(value_states, 'ctx', axis=0, tiled=True)  33.4 us
    all_gather x1, blocking collectives, on_device(): lax.all_gather(delta_rows, 'ctx', axis=0, tiled=True)  30.6 us
    all_gather x1, blocking collectives, on_device(): lax.all_gather(norm_rows, 'ctx', axis=0, tiled=True)  30.6 us
    dot_general x8, matrix products, tile_grads(): jnp.einsum('qgd,kd->gqk', query_blk, key_blk, preferred_element_type=jnp....  10.2 us
    dot_general x4, matrix products, compute(): jnp.einsum('gqk,qgd->kd', prob_b, grad_blk, preferred_element_type=jnp.fl...  6.56 us
    and x8, other arithmetic, tile_grads(): query_live[:, None] & key_live[None, :]  6.44 us
  transfers between devices with their start and end apart: 3, of which 1 were waited for; matrix products, arithmetic and copies ran while one was open for 12% of the time, Pallas kernels for 0%

commit v1 on v0

v1 whole, which is shorter than its diff:
```python
import functools
import math

import jax
import jax.numpy as jnp
from jax import lax
from jax.experimental import pallas as pl
from jax.experimental.pallas import tpu as pltpu
from jax.sharding import PartitionSpec as P

BLOCK = 64
LOG2E = math.log2(math.e)
F32 = jnp.float32
BF16 = jnp.bfloat16
NT = (((1,), (1,)), ((), ()))
TN = (((0,), (0,)), ((), ()))


def dot(a, b, dims=(((1,), (0,)), ((), ()))):
    return lax.dot_general(a, b, dims, preferred_element_type=F32)


def kernel(
    zs, nx, ns,
    q_ref, k_ref, v_ref, o_ref, do_ref, lse_ref, cnt_ref, wq_hbm, wk_hbm, wv_hbm,
    out_ref, dk_ref, dv_ref,
    wq, wkv, qs, dos, lse2, delta, dqt, gq, gkv, acc, kv, part, psend, prcv, fsend, frcv,
    pre, tsend, trcv, xsend, xrcv,
    w_sem, own_send, pair_send, rel_send, kv_recv, p_send, p_recv, f_send, f_recv,
    t_send, t_recv, x_send, x_recv,
):
    cap, dim = k_ref.shape
    group = q_ref.shape[1] // dim
    scale = 1.0 / math.sqrt(dim)
    me = lax.axis_index("ctx")
    y = lax.rem(me, 2)
    z = lax.div(me, 2)
    pair = me + 1 - 2 * y
    h = lax.axis_index("heads")
    core = lax.rem(h, 2)
    x = lax.div(h, 2)
    other = h + 1 - 2 * core
    across = [2 * lax.rem(x + dx, nx) + core for dx in range(nx)]

    w_copies = [
        pltpu.make_async_copy(wq_hbm, wq, w_sem.at[0]),
        pltpu.make_async_copy(wk_hbm, wkv.at[:, pl.ds(0, dim)], w_sem.at[1]),
        pltpu.make_async_copy(wv_hbm, wkv.at[:, pl.ds(dim, dim)], w_sem.at[2]),
    ]

    def remote(src, dst, send, recv, **device):
        return pltpu.make_async_remote_copy(
            src_ref=src, dst_ref=dst, send_sem=send, recv_sem=recv,
            device_id=device, device_id_type=pl.DeviceIdType.MESH,
        )

    barrier = pltpu.get_barrier_semaphore()

    def greet(**device):
        pl.semaphore_signal(
            barrier, inc=1, device_id=device, device_id_type=pl.DeviceIdType.MESH
        )

    def greet_line(z2, _):
        @pl.when(z2 != z)
        def _():
            greet(ctx=2 * z2 + y)
        return 0

    lax.fori_loop(0, zs, greet_line, 0)
    greet(ctx=pair)
    greet(heads=other)
    for dx in range(1, nx):
        greet(heads=across[dx])
    for copy in w_copies:
        copy.start()
    pl.semaphore_wait(barrier, zs + nx)

    own = (k_ref, v_ref)

    def own_copy(t, z2):
        return remote(own[t], kv.at[t, me], own_send.at[t, z2], kv_recv.at[t, me], ctx=2 * z2 + y)

    def pair_copy(t):
        return remote(own[t], kv.at[t, me], pair_send.at[t], kv_recv.at[t, me], ctx=pair)

    def relay_copy(t, z1):
        b = 2 * z1 + y
        return remote(kv.at[t, b], kv.at[t, b], rel_send.at[t, z1], kv_recv.at[t, b], ctx=pair)

    def arrived(b):
        for t in range(2):
            remote(kv.at[t, b], kv.at[t, b], pair_send.at[t], kv_recv.at[t, b], ctx=pair).wait_recv()

    def part_copy(z1):
        return remote(psend.at[z1], prcv.at[z1], p_send.at[z1], p_recv.at[z1], ctx=pair)

    def fin_copy(z1):
        return remote(fsend.at[z1], frcv.at[z], f_send.at[z1], f_recv.at[z], ctx=2 * z1 + y)

    def fin_wait(z2):
        remote(fsend.at[z2], frcv.at[z2], f_send.at[z2], f_recv.at[z2], ctx=2 * z2 + y).wait_recv()

    @pl.when(y == 0)
    def _():
        for t in range(2):
            pair_copy(t).start()

    def push_own(i, _):
        z2 = zs - 1 - i

        @pl.when(z2 > z)
        def _():
            for t in range(2):
                own_copy(t, z2).start()
        return 0

    lax.fori_loop(0, zs, push_own, 0)

    ones = jnp.ones((8, dim), F32)
    lane = lax.broadcasted_iota(jnp.int32, (1, group * cap), 1)
    row = lax.rem(lane, cap)
    alive = row < cnt_ref[me] * BLOCK
    for g in range(group):
        cols = slice(g * dim, (g + 1) * dim)
        qs[g * cap:(g + 1) * cap, :] = q_ref[:, cols]
        dos[g * cap:(g + 1) * cap, :] = do_ref[:, cols]
    prod = jnp.concatenate(
        [
            do_ref[:, g * dim:(g + 1) * dim].astype(F32) * o_ref[:, g * dim:(g + 1) * dim].astype(F32)
            for g in range(group)
        ],
        axis=0,
    )
    delta[...] = lax.dot_general(
        ones, prod, NT, preferred_element_type=F32, precision=lax.Precision.HIGHEST
    )[0:1]
    lse_row = jnp.concatenate([lse_ref[g:g + 1, :] for g in range(group)], axis=1)
    lse2[...] = jnp.where(alive, lse_row * LOG2E, 1e30)

    key_row = lax.broadcasted_iota(jnp.int32, (cap, group * cap), 0)

    def tile(key, value, b, diagonal):
        scores = dot(key, qs[...], NT)
        prob_grad = dot(value, dos[...], NT)
        visible = key_row < cnt_ref[b] * BLOCK
        if diagonal:
            visible = visible & (key_row <= row)
        prob = jnp.where(visible, jnp.exp2(scores * (scale * LOG2E) - lse2[...]), 0.0)
        grad = (prob * (prob_grad - delta[...])).astype(BF16)
        d_value = dot(prob.astype(BF16), dos[...])
        d_key = dot(grad, qs[...])
        terms = dot(key, grad, TN)
        if diagonal:
            dqt[...] = terms
        else:
            dqt[...] += terms
        return d_key, d_value

    d_key, d_value = tile(k_ref[...], v_ref[...], me, True)
    acc[0] = d_key
    acc[1] = d_value

    def pair_tile(z1):
        b = 2 * z1 + 1 - y
        arrived(b)
        d_key, d_value = tile(kv[0, b], kv[1, b], b, False)
        psend[z1, 0] = d_key.astype(BF16)
        psend[z1, 1] = d_value.astype(BF16)
        part_copy(z1).start()

    def combine(z1):
        part_copy(z1).wait_recv()
        fsend[z1] = (part[z1] + prcv[z1].astype(F32)).astype(BF16)
        fin_copy(z1).start()

    def step(i, _):
        z1 = z - i

        @pl.when((z1 >= 0) & (i > 0))
        def _():
            b = 2 * z1 + y
            arrived(b)
            for t in range(2):
                relay_copy(t, z1).start()
            d_key, d_value = tile(kv[0, b], kv[1, b], b, False)
            part[z1, 0] = d_key
            part[z1, 1] = d_value

        @pl.when((z1 >= 0) & ((i > 0) | (y == 1)))
        def _():
            pair_tile(z1)

        @pl.when((z1 >= -1) & (i > 1))
        def _():
            combine(z1 + 1)
        return 0

    lax.fori_loop(0, zs + 1, step, 0)

    query_grad = (jnp.transpose(dqt[...]) * scale).astype(BF16)
    for g in range(group):
        gq[:, g * dim:(g + 1) * dim] = query_grad[g * cap:(g + 1) * cap, :]
    for copy in w_copies:
        copy.wait()
    width = pre.shape[2]

    def project(i, _):
        pre[i] = dot(gq[...], wq[pl.ds(pl.multiple_of(i * width, width), width), :], NT)
        return 0

    lax.fori_loop(0, pre.shape[0], project, 0)

    @pl.when(y == 0)
    def _():
        part_copy(z).wait_recv()
        acc[...] += prcv[z].astype(F32)

    def collect(z2, _):
        @pl.when(z2 > z)
        def _():
            fin_wait(z2)
            acc[...] += frcv[z2].astype(F32)
        return 0

    lax.fori_loop(0, zs, collect, 0)
    key_total = acc[0] * scale
    value_total = acc[1]
    dk_ref[...] = key_total
    dv_ref[...] = value_total
    gkv[:, 0:dim] = key_total.astype(BF16)
    gkv[:, dim:2 * dim] = value_total.astype(BF16)

    def whole(owner, s):
        i = owner * ns + s
        return pre[i] + dot(gkv[...], wkv[pl.ds(pl.multiple_of(i * width, width), width), :], NT)

    def chip_copy(dx, s):
        return remote(tsend.at[dx, s], trcv.at[dx, s], t_send.at[dx, s], t_recv.at[dx, s], heads=other)

    def cross_copy(dx, s):
        return remote(xsend.at[dx, s], xrcv.at[dx, s], x_send.at[dx, s], x_recv.at[dx, s], heads=across[dx])

    order = list(range(1, nx)) + [0]
    for dx in order:
        for s in range(ns):
            tsend[dx, s] = whole(across[dx] + 1 - 2 * core, s).astype(BF16)
            chip_copy(dx, s).start()
        if dx > 0:
            for s in range(ns):
                mine = whole(across[dx], s)
                chip_copy(dx, s).wait_recv()
                xsend[dx, s] = (mine + trcv[dx, s].astype(F32)).astype(BF16)
                cross_copy(dx, s).start()
    for s in range(ns):
        total = whole(h, s)
        chip_copy(0, s).wait_recv()
        total = total + trcv[0, s].astype(F32)
        for dx in range(1, nx):
            cross_copy(dx, s).wait_recv()
            total = total + xrcv[dx, s].astype(F32)
        out_ref[:, s * width:(s + 1) * width] = total.astype(BF16)

    @pl.when(y == 0)
    def _():
        for t in range(2):
            pair_copy(t).wait_send()

    @pl.when(y == 1)
    def _():
        part_copy(z).wait_send()

    def drain(z2, _):
        @pl.when(z2 > z)
        def _():
            for t in range(2):
                own_copy(t, z2).wait_send()

        @pl.when(z2 < z)
        def _():
            for t in range(2):
                relay_copy(t, z2).wait_send()
            part_copy(z2).wait_send()
            fin_copy(z2).wait_send()
        return 0

    lax.fori_loop(0, zs, drain, 0)
    for dx in range(nx):
        for s in range(ns):
            chip_copy(dx, s).wait_send()
            if dx > 0:
                cross_copy(dx, s).wait_send()


def on_device(
    n, nh, queries, key_states, value_states, attention_out, out_grad, log_sum_exp, block_counts,
    w_query, w_key, w_value,
):
    zs, nx, ns = n // 2, nh // 2, 4
    cap, dim = key_states.shape
    width = queries.shape[1]
    rows = width // dim * cap
    model = w_query.shape[0]
    mine = model // nh
    chunk = mine // ns
    vmem = pl.BlockSpec(memory_space=pltpu.VMEM)
    hbm = pl.BlockSpec(memory_space=pl.ANY)
    dma = pltpu.SemaphoreType.DMA
    out, dk, dv = pl.pallas_call(
        functools.partial(kernel, zs, nx, ns),
        out_shape=(
            jax.ShapeDtypeStruct((cap, mine), BF16),
            jax.ShapeDtypeStruct((cap, dim), F32),
            jax.ShapeDtypeStruct((cap, dim), F32),
        ),
        in_specs=[vmem] * 6 + [pl.BlockSpec(memory_space=pltpu.SMEM)] + [hbm] * 3,
        out_specs=(vmem, vmem, vmem),
        scratch_shapes=[
            pltpu.VMEM((model, width), BF16),
            pltpu.VMEM((model, 2 * dim), BF16),
            pltpu.VMEM((rows, dim), BF16),
            pltpu.VMEM((rows, dim), BF16),
            pltpu.VMEM((1, rows), F32),
            pltpu.VMEM((1, rows), F32),
            pltpu.VMEM((dim, rows), F32),
            pltpu.VMEM((cap, width), BF16),
            pltpu.VMEM((cap, 2 * dim), BF16),
            pltpu.VMEM((2, cap, dim), F32),
            pltpu.VMEM((2, n, cap, dim), BF16),
            pltpu.VMEM((zs, 2, cap, dim), F32),
            pltpu.VMEM((zs, 2, cap, dim), BF16),
            pltpu.VMEM((zs, 2, cap, dim), BF16),
            pltpu.VMEM((zs, 2, cap, dim), BF16),
            pltpu.VMEM((zs, 2, cap, dim), BF16),
            pltpu.VMEM((nh * ns, cap, chunk), F32),
            pltpu.VMEM((nx, ns, cap, chunk), BF16),
            pltpu.VMEM((nx, ns, cap, chunk), BF16),
            pltpu.VMEM((nx, ns, cap, chunk), BF16),
            pltpu.VMEM((nx, ns, cap, chunk), BF16),
            dma((3,)),
            dma((2, zs)),
            dma((2,)),
            dma((2, zs)),
            dma((2, n)),
            dma((zs,)),
            dma((zs,)),
            dma((zs,)),
            dma((zs,)),
            dma((nx, ns)),
            dma((nx, ns)),
            dma((nx, ns)),
            dma((nx, ns)),
        ],
        compiler_params=pltpu.CompilerParams(
            collective_id=0, has_side_effects=True, vmem_limit_bytes=52 * 1024 * 1024
        ),
    )(
        queries, key_states, value_states, attention_out, out_grad, log_sum_exp, block_counts,
        w_query, w_key, w_value,
    )
    return out, dk, dv


def solution(mesh):
    return jax.shard_map(
        functools.partial(on_device, mesh.shape["ctx"], mesh.shape["heads"]),
        mesh=mesh,
        in_specs=(
            P("ctx", "heads"),
            P("ctx", "heads"),
            P("ctx", "heads"),
            P("ctx", "heads"),
            P("ctx", "heads"),
            P("heads", "ctx"),
            P(),
            P(None, "heads"),
            P(None, "heads"),
            P(None, "heads"),
        ),
        out_specs=(P("ctx", "heads"), P("ctx", "heads"), P("ctx", "heads")),
        check_vma=False,
    )
```

time: 255 us -> 57.4 us (0.23)
  blocking collectives: 129 us -> 0 us
  Pallas kernels: 0 us -> 48.7 us
  waiting for transfers between devices: 40.8 us -> 0 us
  matrix products: 35.5 us -> 0 us
  other arithmetic: 18 us -> 0 us
  between operations: 13.9 us -> 0.66 us
  local copies, waits for them, and re-layouts: 16 us -> 7.74 us
    all_gather x4 -> x0, blocking collectives: 129 us -> none  [the longest x1 34.2 us: on_device(): key_piece = lax.all_gather(key_states, 'ctx', axis=0, tiled=True)]
    pallas_call x0 -> x1, Pallas kernels: none -> 48.7 us  [on_device(): pl.pallas_call(functools.partial(kernel, zs, nx, ns), out_shape=(jax.Shap...]
    reduce_scatter x1 -> x0, waiting for transfers between devices: 39.4 us -> none  [on_device(): lax.psum_scatter(partial_input, 'heads', scatter_dimension=1, tiled=True)]
    dot_general x23 -> x0, matrix products: 35.5 us -> none  [the longest x8 10.2 us: tile_grads(): jnp.einsum('qgd,kd->gqk', query_blk, key_blk, preferred_element_type=jnp....]
    reduce_sum x10 -> x0, other arithmetic: 6.73 us -> none  [the longest x8 5.73 us: row_info(): length = jnp.sum(jnp.where(onehot, lengths[None, :], 0), axis=1)]
    and x8 -> x0, other arithmetic: 6.44 us -> none  [tile_grads(): query_live[:, None] & key_live[None, :]]
    dynamic_slice x12 -> x0, local copies, waits for them, and re-layouts: 6.38 us -> none  [the longest x8 5.53 us: step(): lax.dynamic_slice_in_dim(grad_piece, begin_row, fold_span, 0)]
    transpose x4 -> x0, local copies, waits for them, and re-layouts: 5.21 us -> none  [tile_grads(): score_grad = probability * (prob_grad - delta_blk.T[:, :, None])]
  transfers between devices with their start and end apart: 3 -> 0, of which waited for: 1 -> 0; matrix products, arithmetic and copies ran while one was open for 12% -> 0% of each run, Pallas kernels for 0% -> 0%
where the time goes in v1:
time: 57.4 us; the launch traced here: 57.1 us
  Pallas kernels  48.7 us (85%)
  local copies, waits for them, and re-layouts  7.74 us (13%)
  between operations  0.66 us (1%)
    pallas_call x1, Pallas kernels, on_device(): pl.pallas_call(functools.partial(kernel, zs, nx, ns), out_shape=(jax.Shap...  48.7 us
    unnamed x17, local copies, waits for them, and re-layouts  7.74 us

profile of v1, /device:TPU:0, one launch (start us, length us, event | category | flops | bytes accessed | tf_op | source)
XLA Modules:
  0.0 57.1 jit_solution(16680947164779237290)
XLA Ops:
  0.6 0.0 copy-start
  0.6 0.9 %copy-done = bf16[192,512]{1,0:T(8,128)(2,1)S(1)} copy-done((bf16[192,512]{1,0:T(8,128)(2,1)S(1)}, bf16[192,512]{1,0:T(8,128)(2,1)}, u32[]{:S(2)}) %copy-start) | copy-done | bytes 196632
  1.6 0.0 copy-start.1
  1.6 0.9 %copy-done.1 = bf16[192,512]{1,0:T(8,128)(2,1)S(1)} copy-done((bf16[192,512]{1,0:T(8,128)(2,1)S(1)}, bf16[192,512]{1,0:T(8,128)(2,1)}, u32[]{:S(2)}) %copy-start.1) | copy-done | bytes 196632
  2.5 0.0 copy-start.2
  2.5 0.9 %copy-done.2 = bf16[192,512]{1,0:T(8,128)(2,1)S(1)} copy-done((bf16[192,512]{1,0:T(8,128)(2,1)S(1)}, bf16[192,512]{1,0:T(8,128)(2,1)}, u32[]{:S(2)}) %copy-start.2) | copy-done | bytes 196632
  3.4 0.0 copy-start.3
  3.4 0.8 %copy-done.3 = bf16[192,128]{1,0:T(8,128)(2,1)S(1)} copy-done((bf16[192,128]{1,0:T(8,128)(2,1)S(1)}, bf16[192,128]{1,0:T(8,128)(2,1)}, u32[]{:S(2)}) %copy-start.3) | copy-done | bytes 49176
  4.2 0.0 copy-start.4
  4.2 0.8 %copy-done.4 = bf16[192,128]{1,0:T(8,128)(2,1)S(1)} copy-done((bf16[192,128]{1,0:T(8,128)(2,1)S(1)}, bf16[192,128]{1,0:T(8,128)(2,1)}, u32[]{:S(2)}) %copy-start.4) | copy-done | bytes 49176
  5.0 0.0 copy-start.5
  5.0 0.7 %copy-done.5 = f32[4,192]{1,0:T(4,128)S(1)} copy-done((f32[4,192]{1,0:T(4,128)S(1)}, f32[4,192]{1,0:T(4,128)}, u32[]{:S(2)}) %copy-start.5) | copy-done | bytes 3096
  5.7 0.0 copy-start.6
  5.7 0.7 %copy-done.6 = s32[8]{0:T(128)S(1)} copy-done((s32[8]{0:T(128)S(1)}, s32[8]{0:T(128)}, u32[]{:S(2)}) %copy-start.6) | copy-done | bytes 56
  6.4 48.7 %shard_map.121 = (bf16[192,1024]{1,0:T(8,128)(2,1)S(1)}, f32[192,128]{1,0:T(8,128)S(1)}, f32[192,128]{1,0:T(8,128)S(1)}) custom-call(bf16[192,512]{1,0:T(8,128)(2,1)S(1)} %copy-done, bf16[192,128]{1,0:T(8,128)(2,1)S(1)} %copy-done.3, bf16[192,128]{1,0:T(8,128)(2,1)S(1)} %copy-done.4, bf16[192,512]{1,0:T(8,128)(2,1)S(1)} %copy-done.1, ...), custom_call_target="tpu_custom_call" | custom-call | tf_op jit(solution)/shard_map/pallas_call | solution.py:309
  55.1 0.7 %copy.16 = bf16[192,1024]{1,0:T(8,128)(2,1)} copy(bf16[192,1024]{1,0:T(8,128)(2,1)S(1)} %get-tuple-element.6) | data formatting | bytes 786432
  55.8 0.6 %copy.17 = f32[192,128]{1,0:T(8,128)} copy(f32[192,128]{1,0:T(8,128)S(1)} %get-tuple-element.7) | data formatting | bytes 196608
  56.5 0.6 %copy.18 = f32[192,128]{1,0:T(8,128)} copy(f32[192,128]{1,0:T(8,128)S(1)} %get-tuple-element.8) | data formatting | bytes 196608
Async XLA Ops:
  0.6 0.9 %copy-start = (bf16[192,512]{1,0:T(8,128)(2,1)S(1)}, bf16[192,512]{1,0:T(8,128)(2,1)}, u32[]{:S(2)}) copy-start(bf16[192,512]{1,0:T(8,128)(2,1)} %q_ref.1) | copy-start | bytes 589828
  1.6 0.9 %copy-start.1 = (bf16[192,512]{1,0:T(8,128)(2,1)S(1)}, bf16[192,512]{1,0:T(8,128)(2,1)}, u32[]{:S(2)}) copy-start(bf16[192,512]{1,0:T(8,128)(2,1)} %o_ref.1) | copy-start | bytes 589828
  2.5 0.9 %copy-start.2 = (bf16[192,512]{1,0:T(8,128)(2,1)S(1)}, bf16[192,512]{1,0:T(8,128)(2,1)}, u32[]{:S(2)}) copy-start(bf16[192,512]{1,0:T(8,128)(2,1)} %do_ref.1) | copy-start | bytes 589828
  3.4 0.8 %copy-start.3 = (bf16[192,128]{1,0:T(8,128)(2,1)S(1)}, bf16[192,128]{1,0:T(8,128)(2,1)}, u32[]{:S(2)}) copy-start(bf16[192,128]{1,0:T(8,128)(2,1)} %k_ref.1) | copy-start | bytes 147460
  4.2 0.8 %copy-start.4 = (bf16[192,128]{1,0:T(8,128)(2,1)S(1)}, bf16[192,128]{1,0:T(8,128)(2,1)}, u32[]{:S(2)}) copy-start(bf16[192,128]{1,0:T(8,128)(2,1)} %v_ref.1) | copy-start | bytes 147460
  5.0 0.7 %copy-start.5 = (f32[4,192]{1,0:T(4,128)S(1)}, f32[4,192]{1,0:T(4,128)}, u32[]{:S(2)}) copy-start(f32[4,192]{1,0:T(4,128)} %lse_ref.1) | copy-start | bytes 9220
  5.7 0.7 %copy-start.6 = (s32[8]{0:T(128)S(1)}, s32[8]{0:T(128)}, u32[]{:S(2)}) copy-start(s32[8]{0:T(128)} %cnt_ref.1) | copy-start | bytes 100

commit v2 on v1

v2 whole, which is shorter than its diff:
```python
import functools
import math

import jax
import jax.numpy as jnp
from jax import lax
from jax.experimental import pallas as pl
from jax.experimental.pallas import tpu as pltpu
from jax.sharding import PartitionSpec as P

BLOCK = 64
LOG2E = math.log2(math.e)
F32 = jnp.float32
BF16 = jnp.bfloat16
NT = (((1,), (1,)), ((), ()))
TN = (((0,), (0,)), ((), ()))


def dot(a, b, dims=(((1,), (0,)), ((), ()))):
    return lax.dot_general(a, b, dims, preferred_element_type=F32)


def kernel(
    zs, nx, ns,
    q_hbm, k_hbm, v_hbm, o_hbm, do_hbm, lse_hbm, cnt_ref, wq_hbm, wk_hbm, wv_hbm,
    out_ref, dk_ref, dv_ref,
    q_ref, k_ref, v_ref, o_ref, do_ref, lse_ref, pair_q, pair_do, wq, wkv, qs, dos, lse2, delta, dqt,
    dq_send, dq_recv, gq, gkv, acc, kv, part, fsend, frcv, hold, tsend, trcv, xsend, xrcv,
    in_sem, w_sem, own_send, kv_recv, swap_send, swap_recv, f_send, f_recv,
    t_send, t_recv, x_send, x_recv,
):
    cap, dim = k_ref.shape
    group = q_ref.shape[1] // dim
    scale = 1.0 / math.sqrt(dim)
    me = lax.axis_index("ctx")
    y = lax.rem(me, 2)
    z = lax.div(me, 2)
    pair = me + 1 - 2 * y
    h = lax.axis_index("heads")
    core = lax.rem(h, 2)
    x = lax.div(h, 2)
    other = h + 1 - 2 * core
    across = [2 * lax.rem(x + dx, nx) + core for dx in range(nx)]

    in_copies = [
        pltpu.make_async_copy(src, dst, in_sem.at[i])
        for i, (src, dst) in enumerate((
            (k_hbm, k_ref), (v_hbm, v_ref), (q_hbm, q_ref), (do_hbm, do_ref), (o_hbm, o_ref),
            (lse_hbm, lse_ref),
        ))
    ]
    for copy in in_copies:
        copy.start()
    w_copies = [
        pltpu.make_async_copy(wq_hbm, wq, w_sem.at[0]),
        pltpu.make_async_copy(wk_hbm, wkv.at[:, pl.ds(0, dim)], w_sem.at[1]),
        pltpu.make_async_copy(wv_hbm, wkv.at[:, pl.ds(dim, dim)], w_sem.at[2]),
    ]

    def remote(src, dst, send, recv, **device):
        return pltpu.make_async_remote_copy(
            src_ref=src, dst_ref=dst, send_sem=send, recv_sem=recv,
            device_id=device, device_id_type=pl.DeviceIdType.MESH,
        )

    barrier = pltpu.get_barrier_semaphore()

    def greet(**device):
        pl.semaphore_signal(
            barrier, inc=1, device_id=device, device_id_type=pl.DeviceIdType.MESH
        )

    def greet_line(z2, _):
        @pl.when(z2 != z)
        def _():
            greet(ctx=2 * z2 + y)
        return 0

    lax.fori_loop(0, zs, greet_line, 0)
    greet(ctx=pair)
    greet(heads=other)
    for dx in range(1, nx):
        greet(heads=across[dx])
    for copy in in_copies:
        copy.wait()
    for copy in w_copies:
        copy.start()
    with jax.named_scope("barrier"):
        pl.semaphore_wait(barrier, zs + nx)

    own = (k_ref, v_ref)

    def own_copy(t, z2):
        return remote(own[t], kv.at[t, z], own_send.at[t, z2], kv_recv.at[t, z], ctx=2 * z2 + y)

    def arrived(z1):
        for t in range(2):
            remote(
                kv.at[t, z1], kv.at[t, z1], own_send.at[t, z1], kv_recv.at[t, z1], ctx=pair
            ).wait_recv()

    swaps = [
        remote(src, dst, swap_send.at[i], swap_recv.at[i], ctx=pair)
        for i, (src, dst) in enumerate((
            (q_ref, pair_q), (do_ref, pair_do), (lse2.at[0], lse2.at[1]), (delta.at[0], delta.at[1]),
            (dq_send, dq_recv),
        ))
    ]

    def fin_copy(z1):
        return remote(fsend.at[z1], frcv.at[z], f_send.at[z1], f_recv.at[z], ctx=2 * z1 + y)

    def fin_wait(z2):
        remote(fsend.at[z2], frcv.at[z2], f_send.at[z2], f_recv.at[z2], ctx=2 * z2 + y).wait_recv()

    swaps[0].start()
    swaps[1].start()

    def push_own(i, _):
        z2 = zs - 1 - i

        @pl.when(z2 > z)
        def _():
            for t in range(2):
                own_copy(t, z2).start()
        return 0

    lax.fori_loop(0, zs, push_own, 0)

    lane = lax.broadcasted_iota(jnp.int32, (1, group * cap), 1)
    row = lax.rem(lane, cap)
    alive = row < cnt_ref[me] * BLOCK
    prod = jnp.concatenate(
        [
            do_ref[:, g * dim:(g + 1) * dim].astype(F32) * o_ref[:, g * dim:(g + 1) * dim].astype(F32)
            for g in range(group)
        ],
        axis=0,
    )
    delta[0] = lax.dot_general(
        jnp.ones((8, dim), F32), prod, NT,
        preferred_element_type=F32, precision=lax.Precision.HIGHEST,
    )[0:1]
    lse_row = jnp.concatenate([lse_ref[g:g + 1, :] for g in range(group)], axis=1)
    lse2[0] = jnp.where(alive, lse_row * LOG2E, 1e30)

    def stack(who, q, do):
        for g in range(group):
            cols = slice(g * dim, (g + 1) * dim)
            qs[who, g * cap:(g + 1) * cap, :] = q[:, cols]
            dos[who, g * cap:(g + 1) * cap, :] = do[:, cols]

    stack(0, q_ref, do_ref)
    swaps[2].start()
    swaps[3].start()
    key_row = lax.broadcasted_iota(jnp.int32, (cap, group * cap), 0)

    def tile(who, key, value, b, diagonal):
        scores = dot(key, qs[who], NT)
        prob_grad = dot(value, dos[who], NT)
        visible = key_row < cnt_ref[b] * BLOCK
        if diagonal:
            visible = visible & (key_row <= row)
        prob = jnp.where(visible, jnp.exp2(scores * (scale * LOG2E) - lse2[who]), 0.0)
        grad = (prob * (prob_grad - delta[who])).astype(BF16)
        d_value = dot(prob.astype(BF16), dos[who])
        d_key = dot(grad, qs[who])
        terms = dot(key, grad, TN)
        if diagonal:
            dqt[who] = terms
        else:
            dqt[who] += terms
        return d_key, d_value

    with jax.named_scope("diag"):
        d_key, d_value = tile(0, k_ref[...], v_ref[...], me, True)
        acc[0] = d_key
        acc[1] = d_value
    dqt[1] = jnp.zeros_like(dqt[1])

    def own_step(z1, _):
        @pl.when(z1 < z)
        def _():
            with jax.named_scope("wait_kv"):
                arrived(z1)
            with jax.named_scope("own_tile"):
                d_key, d_value = tile(0, kv[0, z1], kv[1, z1], 2 * z1 + y, False)
                part[z1, 0] = d_key
                part[z1, 1] = d_value
        return 0

    lax.fori_loop(0, zs, own_step, 0)
    with jax.named_scope("wait_swap"):
        for copy in swaps[:4]:
            copy.wait_recv()
    stack(1, pair_q, pair_do)

    def pair_step(z1, _):
        @pl.when(z1 < z)
        def _():
            with jax.named_scope("pair_tile"):
                d_key, d_value = tile(1, kv[0, z1], kv[1, z1], 2 * z1 + y, False)
                fsend[z1, 0] = (part[z1, 0] + d_key).astype(BF16)
                fsend[z1, 1] = (part[z1, 1] + d_value).astype(BF16)
            fin_copy(z1).start()
        return 0

    lax.fori_loop(0, zs, pair_step, 0)

    @pl.when(y == 0)
    def _():
        with jax.named_scope("pair_own"):
            d_key, d_value = tile(1, k_ref[...], v_ref[...], me, False)
            acc[0] += d_key
            acc[1] += d_value

    dq_send[...] = dqt[1].astype(BF16)
    swaps[4].start()

    def collect(i, _):
        z2 = zs - 1 - i

        @pl.when(z2 > z)
        def _():
            fin_wait(z2)
            acc[...] += frcv[z2].astype(F32)
        return 0

    with jax.named_scope("collect"):
        lax.fori_loop(0, zs, collect, 0)
    key_total = acc[0] * scale
    value_total = acc[1]
    dk_ref[...] = key_total
    dv_ref[...] = value_total
    gkv[:, 0:dim] = key_total.astype(BF16)
    gkv[:, dim:2 * dim] = value_total.astype(BF16)
    with jax.named_scope("wait_dq"):
        swaps[4].wait_recv()
    query_grad = (jnp.transpose(dqt[0] + dq_recv[...].astype(F32)) * scale).astype(BF16)
    for g in range(group):
        gq[:, g * dim:(g + 1) * dim] = query_grad[g * cap:(g + 1) * cap, :]
    for copy in w_copies:
        copy.wait()
    width = hold.shape[2]

    def whole(owner, s):
        rows = pl.ds(pl.multiple_of((owner * ns + s) * width, width), width)
        return dot(gq[...], wq[rows, :], NT) + dot(gkv[...], wkv[rows, :], NT)

    def chip_copy(dx, s):
        return remote(tsend.at[dx, s], trcv.at[dx, s], t_send.at[dx, s], t_recv.at[dx, s], heads=other)

    def cross_copy(dx, s):
        return remote(xsend.at[dx, s], xrcv.at[dx, s], x_send.at[dx, s], x_recv.at[dx, s], heads=across[dx])

    def give(dx, s):
        tsend[dx, s] = whole(across[dx] + 1 - 2 * core, s).astype(BF16)
        chip_copy(dx, s).start()

    def cross(dx, s):
        with jax.named_scope("wait_chip"):
            chip_copy(dx, s).wait_recv()
        xsend[dx, s] = (hold[s] + trcv[dx, s].astype(F32)).astype(BF16)
        cross_copy(dx, s).start()

    for dx in range(1, nx):
        for s in range(ns):
            give(dx, s)
            if s > 0:
                cross(dx, s - 1)
            hold[s] = whole(across[dx], s)
        cross(dx, ns - 1)
    for s in range(ns):
        give(0, s)
    for s in range(ns):
        hold[s] = whole(h, s)
    for s in range(ns):
        chip_copy(0, s).wait_recv()
        total = hold[s] + trcv[0, s].astype(F32)
        for dx in range(1, nx):
            with jax.named_scope("wait_cross"):
                cross_copy(dx, s).wait_recv()
            total = total + xrcv[dx, s].astype(F32)
        out_ref[:, s * width:(s + 1) * width] = total.astype(BF16)

    for copy in swaps:
        copy.wait_send()

    def drain(z2, _):
        @pl.when(z2 > z)
        def _():
            for t in range(2):
                own_copy(t, z2).wait_send()

        @pl.when(z2 < z)
        def _():
            fin_copy(z2).wait_send()
        return 0

    lax.fori_loop(0, zs, drain, 0)
    for dx in range(nx):
        for s in range(ns):
            chip_copy(dx, s).wait_send()
            if dx > 0:
                cross_copy(dx, s).wait_send()


def on_device(
    n, nh, queries, key_states, value_states, attention_out, out_grad, log_sum_exp, block_counts,
    w_query, w_key, w_value,
):
    zs, nx, ns = n // 2, nh // 2, 4
    cap, dim = key_states.shape
    width = queries.shape[1]
    rows = width // dim * cap
    model = w_query.shape[0]
    mine = model // nh
    chunk = mine // ns
    vmem = pl.BlockSpec(memory_space=pltpu.VMEM)
    hbm = pl.BlockSpec(memory_space=pl.ANY)
    dma = pltpu.SemaphoreType.DMA
    out, dk, dv = pl.pallas_call(
        functools.partial(kernel, zs, nx, ns),
        out_shape=(
            jax.ShapeDtypeStruct((cap, mine), BF16),
            jax.ShapeDtypeStruct((cap, dim), F32),
            jax.ShapeDtypeStruct((cap, dim), F32),
        ),
        in_specs=[hbm] * 6 + [pl.BlockSpec(memory_space=pltpu.SMEM)] + [hbm] * 3,
        out_specs=(vmem, vmem, vmem),
        scratch_shapes=[
            pltpu.VMEM((cap, width), BF16),
            pltpu.VMEM((cap, dim), BF16),
            pltpu.VMEM((cap, dim), BF16),
            pltpu.VMEM((cap, width), BF16),
            pltpu.VMEM((cap, width), BF16),
            pltpu.VMEM(log_sum_exp.shape, F32),
            pltpu.VMEM((cap, width), BF16),
            pltpu.VMEM((cap, width), BF16),
            pltpu.VMEM((model, width), BF16),
            pltpu.VMEM((model, 2 * dim), BF16),
            pltpu.VMEM((2, rows, dim), BF16),
            pltpu.VMEM((2, rows, dim), BF16),
            pltpu.VMEM((2, 1, rows), F32),
            pltpu.VMEM((2, 1, rows), F32),
            pltpu.VMEM((2, dim, rows), F32),
            pltpu.VMEM((dim, rows), BF16),
            pltpu.VMEM((dim, rows), BF16),
            pltpu.VMEM((cap, width), BF16),
            pltpu.VMEM((cap, 2 * dim), BF16),
            pltpu.VMEM((2, cap, dim), F32),
            pltpu.VMEM((2, zs, cap, dim), BF16),
            pltpu.VMEM((zs, 2, cap, dim), F32),
            pltpu.VMEM((zs, 2, cap, dim), BF16),
            pltpu.VMEM((zs, 2, cap, dim), BF16),
            pltpu.VMEM((ns, cap, chunk), F32),
            pltpu.VMEM((nx, ns, cap, chunk), BF16),
            pltpu.VMEM((nx, ns, cap, chunk), BF16),
            pltpu.VMEM((nx, ns, cap, chunk), BF16),
            pltpu.VMEM((nx, ns, cap, chunk), BF16),
            dma((6,)),
            dma((3,)),
            dma((2, zs)),
            dma((2, zs)),
            dma((5,)),
            dma((5,)),
            dma((zs,)),
            dma((zs,)),
            dma((nx, ns)),
            dma((nx, ns)),
            dma((nx, ns)),
            dma((nx, ns)),
        ],
        compiler_params=pltpu.CompilerParams(
            collective_id=0, has_side_effects=True, vmem_limit_bytes=52 * 1024 * 1024
        ),
    )(
        queries, key_states, value_states, attention_out, out_grad, log_sum_exp, block_counts,
        w_query, w_key, w_value,
    )
    return out, dk, dv


def solution(mesh):
    return jax.shard_map(
        functools.partial(on_device, mesh.shape["ctx"], mesh.shape["heads"]),
        mesh=mesh,
        in_specs=(
            P("ctx", "heads"),
            P("ctx", "heads"),
            P("ctx", "heads"),
            P("ctx", "heads"),
            P("ctx", "heads"),
            P("heads", "ctx"),
            P(),
            P(None, "heads"),
            P(None, "heads"),
            P(None, "heads"),
        ),
        out_specs=(P("ctx", "heads"), P("ctx", "heads"), P("ctx", "heads")),
        check_vma=False,
    )
```

time: 57.4 us -> 47.2 us (0.82)
  Pallas kernels: 48.7 us -> 38.4 us
    pallas_call x1, Pallas kernels: 48.7 us -> 38.4 us  [on_device(): pl.pallas_call(functools.partial(kernel, zs, nx, ns), out_shape=(jax.Shap...]
where the time goes in v2:
time: 47.2 us; the launch traced here: 46.8 us
  Pallas kernels  38.4 us (81%)
  local copies, waits for them, and re-layouts  7.74 us (16%)
  between operations  0.66 us (1%)
    pallas_call x1, Pallas kernels, on_device(): pl.pallas_call(functools.partial(kernel, zs, nx, ns), out_shape=(jax.Shap...  38.4 us
    unnamed x17, local copies, waits for them, and re-layouts  7.74 us

profile of v2, /device:TPU:0, one launch (start us, length us, event | category | flops | bytes accessed | tf_op | source)
XLA Modules:
  0.0 46.8 jit_solution(2658052400782882833)
XLA Ops:
  0.6 0.0 copy-start
  0.6 0.9 %copy-done = bf16[192,512]{1,0:T(8,128)(2,1)S(1)} copy-done((bf16[192,512]{1,0:T(8,128)(2,1)S(1)}, bf16[192,512]{1,0:T(8,128)(2,1)}, u32[]{:S(2)}) %copy-start) | copy-done | bytes 196632
  1.6 0.0 copy-start.1
  1.6 0.9 %copy-done.1 = bf16[192,512]{1,0:T(8,128)(2,1)S(1)} copy-done((bf16[192,512]{1,0:T(8,128)(2,1)S(1)}, bf16[192,512]{1,0:T(8,128)(2,1)}, u32[]{:S(2)}) %copy-start.1) | copy-done | bytes 196632
  2.5 0.0 copy-start.2
  2.5 0.9 %copy-done.2 = bf16[192,512]{1,0:T(8,128)(2,1)S(1)} copy-done((bf16[192,512]{1,0:T(8,128)(2,1)S(1)}, bf16[192,512]{1,0:T(8,128)(2,1)}, u32[]{:S(2)}) %copy-start.2) | copy-done | bytes 196632
  3.4 0.0 copy-start.3
  3.4 0.8 %copy-done.3 = bf16[192,128]{1,0:T(8,128)(2,1)S(1)} copy-done((bf16[192,128]{1,0:T(8,128)(2,1)S(1)}, bf16[192,128]{1,0:T(8,128)(2,1)}, u32[]{:S(2)}) %copy-start.3) | copy-done | bytes 49176
  4.2 0.0 copy-start.4
  4.2 0.8 %copy-done.4 = bf16[192,128]{1,0:T(8,128)(2,1)S(1)} copy-done((bf16[192,128]{1,0:T(8,128)(2,1)S(1)}, bf16[192,128]{1,0:T(8,128)(2,1)}, u32[]{:S(2)}) %copy-start.4) | copy-done | bytes 49176
  5.0 0.0 copy-start.5
  5.0 0.7 %copy-done.5 = f32[4,192]{1,0:T(4,128)S(1)} copy-done((f32[4,192]{1,0:T(4,128)S(1)}, f32[4,192]{1,0:T(4,128)}, u32[]{:S(2)}) %copy-start.5) | copy-done | bytes 3096
  5.7 0.0 copy-start.6
  5.7 0.7 %copy-done.6 = s32[8]{0:T(128)S(1)} copy-done((s32[8]{0:T(128)S(1)}, s32[8]{0:T(128)}, u32[]{:S(2)}) %copy-start.6) | copy-done | bytes 56
  6.4 38.4 %shard_map.121 = (bf16[192,1024]{1,0:T(8,128)(2,1)S(1)}, f32[192,128]{1,0:T(8,128)S(1)}, f32[192,128]{1,0:T(8,128)S(1)}) custom-call(bf16[192,512]{1,0:T(8,128)(2,1)S(1)} %copy-done, bf16[192,128]{1,0:T(8,128)(2,1)S(1)} %copy-done.3, bf16[192,128]{1,0:T(8,128)(2,1)S(1)} %copy-done.4, bf16[192,512]{1,0:T(8,128)(2,1)S(1)} %copy-done.1, ...), custom_call_target="tpu_custom_call" | custom-call | tf_op jit(solution)/shard_map/pallas_call | solution.py:322
  44.8 0.7 %copy.16 = bf16[192,1024]{1,0:T(8,128)(2,1)} copy(bf16[192,1024]{1,0:T(8,128)(2,1)S(1)} %get-tuple-element.6) | data formatting | bytes 786432
  45.6 0.6 %copy.17 = f32[192,128]{1,0:T(8,128)} copy(f32[192,128]{1,0:T(8,128)S(1)} %get-tuple-element.7) | data formatting | bytes 196608
  46.2 0.6 %copy.18 = f32[192,128]{1,0:T(8,128)} copy(f32[192,128]{1,0:T(8,128)S(1)} %get-tuple-element.8) | data formatting | bytes 196608
Async XLA Ops:
  0.6 0.9 %copy-start = (bf16[192,512]{1,0:T(8,128)(2,1)S(1)}, bf16[192,512]{1,0:T(8,128)(2,1)}, u32[]{:S(2)}) copy-start(bf16[192,512]{1,0:T(8,128)(2,1)} %q_hbm.1) | copy-start | bytes 589828
  1.6 0.9 %copy-start.1 = (bf16[192,512]{1,0:T(8,128)(2,1)S(1)}, bf16[192,512]{1,0:T(8,128)(2,1)}, u32[]{:S(2)}) copy-start(bf16[192,512]{1,0:T(8,128)(2,1)} %o_hbm.1) | copy-start | bytes 589828
  2.5 0.9 %copy-start.2 = (bf16[192,512]{1,0:T(8,128)(2,1)S(1)}, bf16[192,512]{1,0:T(8,128)(2,1)}, u32[]{:S(2)}) copy-start(bf16[192,512]{1,0:T(8,128)(2,1)} %do_hbm.1) | copy-start | bytes 589828
  3.4 0.8 %copy-start.3 = (bf16[192,128]{1,0:T(8,128)(2,1)S(1)}, bf16[192,128]{1,0:T(8,128)(2,1)}, u32[]{:S(2)}) copy-start(bf16[192,128]{1,0:T(8,128)(2,1)} %k_hbm.1) | copy-start | bytes 147460
  4.2 0.8 %copy-start.4 = (bf16[192,128]{1,0:T(8,128)(2,1)S(1)}, bf16[192,128]{1,0:T(8,128)(2,1)}, u32[]{:S(2)}) copy-start(bf16[192,128]{1,0:T(8,128)(2,1)} %v_hbm.1) | copy-start | bytes 147460
  5.0 0.7 %copy-start.5 = (f32[4,192]{1,0:T(4,128)S(1)}, f32[4,192]{1,0:T(4,128)}, u32[]{:S(2)}) copy-start(f32[4,192]{1,0:T(4,128)} %lse_hbm.1) | copy-start | bytes 9220
  5.7 0.7 %copy-start.6 = (s32[8]{0:T(128)S(1)}, s32[8]{0:T(128)}, u32[]{:S(2)}) copy-start(s32[8]{0:T(128)} %cnt_ref.1) | copy-start | bytes 100

commit v3 on v2

--- a/solution.py
+++ b/solution.py
@@ -22,15 +22,17 @@
 
 def kernel(
     zs, nx, ns,
-    q_hbm, k_hbm, v_hbm, o_hbm, do_hbm, lse_hbm, cnt_ref, wq_hbm, wk_hbm, wv_hbm,
+    q_hbm, k_hbm, v_hbm, o_hbm, do_hbm, lse_hbm, cnt_hbm, wq_hbm, wk_hbm, wv_hbm,
     out_ref, dk_ref, dv_ref,
-    q_ref, k_ref, v_ref, o_ref, do_ref, lse_ref, pair_q, pair_do, wq, wkv, qs, dos, lse2, delta, dqt,
-    dq_send, dq_recv, gq, gkv, acc, kv, part, fsend, frcv, hold, tsend, trcv, xsend, xrcv,
+    cnt_ref, q_ref, k_ref, v_ref, o_ref, do_ref, lse_ref, pair_q, pair_do, wq, wkv, qs, dos, lse2, delta, dqt,
+    dq_own, dq_send, dq_recv, gq, gkv, acc, kv, part, fsend, frcv, keep, hold, csend, crcv, tsend, trcv, xsend, xrcv,
     in_sem, w_sem, own_send, kv_recv, swap_send, swap_recv, f_send, f_recv,
-    t_send, t_recv, x_send, x_recv,
+    c_send, c_recv, t_send, t_recv, x_send, x_recv,
 ):
     cap, dim = k_ref.shape
     group = q_ref.shape[1] // dim
+    half = cap // 2
+    np = cap // half
     scale = 1.0 / math.sqrt(dim)
     me = lax.axis_index("ctx")
     y = lax.rem(me, 2)
@@ -46,7 +48,7 @@
         pltpu.make_async_copy(src, dst, in_sem.at[i])
         for i, (src, dst) in enumerate((
             (k_hbm, k_ref), (v_hbm, v_ref), (q_hbm, q_ref), (do_hbm, do_ref), (o_hbm, o_ref),
-            (lse_hbm, lse_ref),
+            (lse_hbm, lse_ref), (cnt_hbm, cnt_ref),
         ))
     ]
     for copy in in_copies:
@@ -103,15 +105,19 @@
         remote(src, dst, swap_send.at[i], swap_recv.at[i], ctx=pair)
         for i, (src, dst) in enumerate((
             (q_ref, pair_q), (do_ref, pair_do), (lse2.at[0], lse2.at[1]), (delta.at[0], delta.at[1]),
-            (dq_send, dq_recv),
+            *((dq_send.at[r], dq_recv.at[r]) for r in range(np)),
         ))
     ]
 
-    def fin_copy(z1):
-        return remote(fsend.at[z1], frcv.at[z], f_send.at[z1], f_recv.at[z], ctx=2 * z1 + y)
-
-    def fin_wait(z2):
-        remote(fsend.at[z2], frcv.at[z2], f_send.at[z2], f_recv.at[z2], ctx=2 * z2 + y).wait_recv()
+    def fin_copy(r, z1):
+        return remote(
+            fsend.at[r, z1], frcv.at[r, z], f_send.at[r, z1], f_recv.at[r, z], ctx=2 * z1 + y
+        )
+
+    def fin_wait(r, z2):
+        remote(
+            fsend.at[r, z2], frcv.at[r, z2], f_send.at[r, z2], f_recv.at[r, z2], ctx=2 * z2 + y
+        ).wait_recv()
 
     swaps[0].start()
     swaps[1].start()
@@ -200,12 +206,26 @@
         def _():
             with jax.named_scope("pair_tile"):
                 d_key, d_value = tile(1, kv[0, z1], kv[1, z1], 2 * z1 + y, False)
-                fsend[z1, 0] = (part[z1, 0] + d_key).astype(BF16)
-                fsend[z1, 1] = (part[z1, 1] + d_value).astype(BF16)
-            fin_copy(z1).start()
+                d_key = (part[z1, 0] + d_key).astype(BF16)
+                d_value = (part[z1, 1] + d_value).astype(BF16)
+                for r in range(np):
+                    fsend[r, z1, 0] = d_key[r * half:(r + 1) * half]
+                    fsend[r, z1, 1] = d_value[r * half:(r + 1) * half]
+            fin_copy(0, z1).start()
         return 0
 
     lax.fori_loop(0, zs, pair_step, 0)
+
+    def later(i, _):
+        r = lax.div(i, zs) + 1
+        z1 = lax.rem(i, zs)
+
+        @pl.when(z1 < z)
+        def _():
+            fin_copy(r, z1).start()
+        return 0
+
+    lax.fori_loop(0, zs * (np - 1), later, 0)
 
     @pl.when(y == 0)
     def _():
@@ -214,74 +234,87 @@
             acc[0] += d_key
             acc[1] += d_value
 
-    dq_send[...] = dqt[1].astype(BF16)
-    swaps[4].start()
-
-    def collect(i, _):
-        z2 = zs - 1 - i
-
-        @pl.when(z2 > z)
-        def _():
-            fin_wait(z2)
-            acc[...] += frcv[z2].astype(F32)
-        return 0
-
-    with jax.named_scope("collect"):
-        lax.fori_loop(0, zs, collect, 0)
-    key_total = acc[0] * scale
-    value_total = acc[1]
-    dk_ref[...] = key_total
-    dv_ref[...] = value_total
-    gkv[:, 0:dim] = key_total.astype(BF16)
-    gkv[:, dim:2 * dim] = value_total.astype(BF16)
-    with jax.named_scope("wait_dq"):
-        swaps[4].wait_recv()
-    query_grad = (jnp.transpose(dqt[0] + dq_recv[...].astype(F32)) * scale).astype(BF16)
-    for g in range(group):
-        gq[:, g * dim:(g + 1) * dim] = query_grad[g * cap:(g + 1) * cap, :]
+    pair_dq = jnp.transpose(dqt[1]).astype(BF16)
+    for r in range(np):
+        for g in range(group):
+            dq_send[r, g] = pair_dq[g * cap + r * half:g * cap + (r + 1) * half]
+        swaps[4 + r].start()
+    dq_own[...] = jnp.transpose(dqt[0])
     for copy in w_copies:
         copy.wait()
     width = hold.shape[2]
 
-    def whole(owner, s):
-        rows = pl.ds(pl.multiple_of((owner * ns + s) * width, width), width)
-        return dot(gq[...], wq[rows, :], NT) + dot(gkv[...], wkv[rows, :], NT)
-
-    def chip_copy(dx, s):
-        return remote(tsend.at[dx, s], trcv.at[dx, s], t_send.at[dx, s], t_recv.at[dx, s], heads=other)
-
-    def cross_copy(dx, s):
-        return remote(xsend.at[dx, s], xrcv.at[dx, s], x_send.at[dx, s], x_recv.at[dx, s], heads=across[dx])
-
-    def give(dx, s):
-        tsend[dx, s] = whole(across[dx] + 1 - 2 * core, s).astype(BF16)
-        chip_copy(dx, s).start()
-
-    def cross(dx, s):
-        with jax.named_scope("wait_chip"):
-            chip_copy(dx, s).wait_recv()
-        xsend[dx, s] = (hold[s] + trcv[dx, s].astype(F32)).astype(BF16)
-        cross_copy(dx, s).start()
-
-    for dx in range(1, nx):
+    def whole(owner, s, rows):
+        cols = pl.ds(pl.multiple_of((owner * ns + s) * width, width), width)
+        return dot(gq[rows, :], wq[cols, :], NT) + dot(gkv[rows, :], wkv[cols, :], NT)
+
+    def chip_copy(s):
+        return remote(csend.at[s], crcv.at[s], c_send.at[s], c_recv.at[s], heads=other)
+
+    def near_copy(dx, r, s):
+        at = (dx, r, s)
+        return remote(tsend.at[at], trcv.at[at], t_send.at[at], t_recv.at[at], heads=other)
+
+    def cross_copy(dx, r, s):
+        at = (dx, r, s)
+        return remote(xsend.at[at], xrcv.at[at], x_send.at[at], x_recv.at[at], heads=across[dx])
+
+    def cross(dx, r, s):
+        with jax.named_scope("wait_near"):
+            near_copy(dx, r, s).wait_recv()
+        xsend[dx, r, s] = (keep[s] + trcv[dx, r, s].astype(F32)).astype(BF16)
+        cross_copy(dx, r, s).start()
+
+    for r in range(np):
+        rows = slice(r * half, (r + 1) * half)
+
+        def collect(i, _):
+            z2 = zs - 1 - i
+
+            @pl.when(z2 > z)
+            def _():
+                fin_wait(r, z2)
+                acc[:, rows, :] += frcv[r, z2].astype(F32)
+            return 0
+
+        with jax.named_scope("wait_dq"):
+            swaps[4 + r].wait_recv()
+        for g in range(group):
+            total = dq_own[g * cap + r * half:g * cap + (r + 1) * half, :] + dq_recv[r, g].astype(F32)
+            gq[rows, g * dim:(g + 1) * dim] = (total * scale).astype(BF16)
+        with jax.named_scope("collect"):
+            lax.fori_loop(0, zs, collect, 0)
+        key_total = acc[0, rows, :] * scale
+        value_total = acc[1, rows, :]
+        dk_ref[rows, :] = key_total
+        dv_ref[rows, :] = value_total
+        gkv[rows, 0:dim] = key_total.astype(BF16)
+        gkv[rows, dim:2 * dim] = value_total.astype(BF16)
+        for dx in range(1, nx):
+            for s in range(ns):
+                tsend[dx, r, s] = whole(across[dx] + 1 - 2 * core, s, rows).astype(BF16)
+                near_copy(dx, r, s).start()
+            for s in range(ns):
+                keep[s] = whole(across[dx], s, rows)
+                cross(dx, r, s)
+    everything = slice(0, cap)
+    for s in range(ns):
+        csend[s] = whole(other, s, everything).astype(BF16)
+        chip_copy(s).start()
+    for s in range(ns):
+        hold[s] = whole(h, s, everything)
+    for s in range(ns):
+        chip_copy(s).wait_recv()
+        hold[s] += crcv[s].astype(F32)
+    for r in range(np):
+        rows = slice(r * half, (r + 1) * half)
         for s in range(ns):
-            give(dx, s)
-            if s > 0:
-                cross(dx, s - 1)
-            hold[s] = whole(across[dx], s)
-        cross(dx, ns - 1)
-    for s in range(ns):
-        give(0, s)
-    for s in range(ns):
-        hold[s] = whole(h, s)
-    for s in range(ns):
-        chip_copy(0, s).wait_recv()
-        total = hold[s] + trcv[0, s].astype(F32)
-        for dx in range(1, nx):
-            with jax.named_scope("wait_cross"):
-                cross_copy(dx, s).wait_recv()
-            total = total + xrcv[dx, s].astype(F32)
-        out_ref[:, s * width:(s + 1) * width] = total.astype(BF16)
+            total = hold[s, rows, :]
+            for dx in range(1, nx):
+                with jax.named_scope("wait_cross"):
+                    cross_copy(dx, r, s).wait_recv()
+                total = total + xrcv[dx, r, s].astype(F32)
+            out_ref[rows, s * width:(s + 1) * width] = total.astype(BF16)
 
     for copy in swaps:
         copy.wait_send()
@@ -294,15 +327,17 @@
 
         @pl.when(z2 < z)
         def _():
-            fin_copy(z2).wait_send()
+            for r in range(np):
+                fin_copy(r, z2).wait_send()
         return 0
 
     lax.fori_loop(0, zs, drain, 0)
-    for dx in range(nx):
-        for s in range(ns):
-            chip_copy(dx, s).wait_send()
-            if dx > 0:
-                cross_copy(dx, s).wait_send()
+    for s in range(ns):
+        chip_copy(s).wait_send()
+        for dx in range(1, nx):
+            for r in range(np):
+                near_copy(dx, r, s).wait_send()
+                cross_copy(dx, r, s).wait_send()
 
 
 def on_device(
@@ -317,18 +352,21 @@
     mine = model // nh
     chunk = mine // ns
     vmem = pl.BlockSpec(memory_space=pltpu.VMEM)
-    hbm = pl.BlockSpec(memory_space=pl.ANY)
+    half = cap // 2
+    np = cap // half
+    hbm = pl.BlockSpec(memory_space=pltpu.HBM)
     dma = pltpu.SemaphoreType.DMA
-    out, dk, dv = pl.pallas_call(
+    results = pl.pallas_call(
         functools.partial(kernel, zs, nx, ns),
         out_shape=(
             jax.ShapeDtypeStruct((cap, mine), BF16),
             jax.ShapeDtypeStruct((cap, dim), F32),
             jax.ShapeDtypeStruct((cap, dim), F32),
         ),
-        in_specs=[hbm] * 6 + [pl.BlockSpec(memory_space=pltpu.SMEM)] + [hbm] * 3,
+        in_specs=[hbm] * 10,
         out_specs=(vmem, vmem, vmem),
         scratch_shapes=[
+            pltpu.SMEM(block_counts.shape, jnp.int32),
             pltpu.VMEM((cap, width), BF16),
             pltpu.VMEM((cap, dim), BF16),
             pltpu.VMEM((cap, dim), BF16),
@@ -344,41 +382,52 @@
             pltpu.VMEM((2, 1, rows), F32),
             pltpu.VMEM((2, 1, rows), F32),
             pltpu.VMEM((2, dim, rows), F32),
-            pltpu.VMEM((dim, rows), BF16),
-            pltpu.VMEM((dim, rows), BF16),
+            pltpu.VMEM((rows, dim), F32),
+            pltpu.VMEM((np, width // dim, half, dim), BF16),
+            pltpu.VMEM((np, width // dim, half, dim), BF16),
             pltpu.VMEM((cap, width), BF16),
             pltpu.VMEM((cap, 2 * dim), BF16),
             pltpu.VMEM((2, cap, dim), F32),
             pltpu.VMEM((2, zs, cap, dim), BF16),
             pltpu.VMEM((zs, 2, cap, dim), F32),
-            pltpu.VMEM((zs, 2, cap, dim), BF16),
-            pltpu.VMEM((zs, 2, cap, dim), BF16),
+            pltpu.VMEM((np, zs, 2, half, dim), BF16),
+            pltpu.VMEM((np, zs, 2, half, dim), BF16),
+            pltpu.VMEM((ns, half, chunk), F32),
             pltpu.VMEM((ns, cap, chunk), F32),
-            pltpu.VMEM((nx, ns, cap, chunk), BF16),
-            pltpu.VMEM((nx, ns, cap, chunk), BF16),
-            pltpu.VMEM((nx, ns, cap, chunk), BF16),
-            pltpu.VMEM((nx, ns, cap, chunk), BF16),
-            dma((6,)),
+            pltpu.VMEM((ns, cap, chunk), BF16),
+            pltpu.VMEM((ns, cap, chunk), BF16),
+            pltpu.VMEM((nx, np, ns, half, chunk), BF16),
+            pltpu.VMEM((nx, np, ns, half, chunk), BF16),
+            pltpu.VMEM((nx, np, ns, half, chunk), BF16),
+            pltpu.VMEM((nx, np, ns, half, chunk), BF16),
+            dma((7,)),
             dma((3,)),
             dma((2, zs)),
             dma((2, zs)),
-            dma((5,)),
-            dma((5,)),
-            dma((zs,)),
-            dma((zs,)),
-            dma((nx, ns)),
-            dma((nx, ns)),
-            dma((nx, ns)),
-            dma((nx, ns)),
+            dma((4 + np,)),
+            dma((4 + np,)),
+            dma((np, zs)),
+            dma((np, zs)),
+            dma((ns,)),
+            dma((ns,)),
+            dma((nx, np, ns)),
+            dma((nx, np, ns)),
+            dma((nx, np, ns)),
+            dma((nx, np, ns)),
         ],
         compiler_params=pltpu.CompilerParams(
             collective_id=0, has_side_effects=True, vmem_limit_bytes=52 * 1024 * 1024
         ),
     )(
-        queries, key_states, value_states, attention_out, out_grad, log_sum_exp, block_counts,
-        w_query, w_key, w_value,
+        *(
+            pltpu.with_memory_space_constraint(a, pltpu.HBM)
+            for a in (
+                queries, key_states, value_states, attention_out, out_grad, log_sum_exp,
+                block_counts, w_query, w_key, w_value,
+            )
+        )
     )
-    return out, dk, dv
+    return results
 
 
 def solution(mesh):

time: 47.2 us -> 38.5 us (0.82)
  local copies, waits for them, and re-layouts: 7.74 us -> 2.03 us
  Pallas kernels: 38.4 us -> 35.7 us
    unnamed x17 -> x3, local copies, waits for them, and re-layouts: 7.74 us -> 2.03 us
    pallas_call x1, Pallas kernels: 38.4 us -> 35.7 us  [on_device(): pl.pallas_call(functools.partial(kernel, zs, nx, ns), out_shape=(jax.Shap...]
where the time goes in v3:
time: 38.5 us; the launch traced here: 38.4 us
  Pallas kernels  35.7 us (93%)
  local copies, waits for them, and re-layouts  2.03 us (5%)
  between operations  0.64 us (2%)
    pallas_call x1, Pallas kernels, on_device(): pl.pallas_call(functools.partial(kernel, zs, nx, ns), out_shape=(jax.Shap...  35.7 us
    unnamed x3, local copies, waits for them, and re-layouts  2.03 us

profile of v3, /device:TPU:0, one launch (start us, length us, event | category | flops | bytes accessed | tf_op | source)
XLA Modules:
  0.0 38.4 jit_solution(10806331241256708731)
XLA Ops:
  0.6 35.7 %shard_map.121 = (bf16[192,1024]{1,0:T(8,128)(2,1)S(1)}, f32[192,128]{1,0:T(8,128)S(1)}, f32[192,128]{1,0:T(8,128)S(1)}) custom-call(bf16[192,512]{1,0:T(8,128)(2,1)} %q_hbm.1, bf16[192,128]{1,0:T(8,128)(2,1)} %k_hbm.1, bf16[192,128]{1,0:T(8,128)(2,1)} %v_hbm.1, bf16[192,512]{1,0:T(8,128)(2,1)} %o_hbm.1, bf16[192,512]{1,0:T(8,128)(2,1)} %do_hbm.1, ...), custom_call_target="tpu_custom_call" | custom-call | tf_op jit(solution)/shard_map/pallas_call | solution.py:359
  36.3 0.7 %copy.16 = bf16[192,1024]{1,0:T(8,128)(2,1)} copy(bf16[192,1024]{1,0:T(8,128)(2,1)S(1)} %get-tuple-element.6) | data formatting | bytes 786432
  37.1 0.6 %copy.17 = f32[192,128]{1,0:T(8,128)} copy(f32[192,128]{1,0:T(8,128)S(1)} %get-tuple-element.7) | data formatting | bytes 196608
  37.7 0.6 %copy.18 = f32[192,128]{1,0:T(8,128)} copy(f32[192,128]{1,0:T(8,128)S(1)} %get-tuple-element.8) | data formatting | bytes 196608
